TPU v7x, 32 devices: a 4x4x1 block of a 4x4x8 slice. The times are simulated.
32 devices in a mesh: dp: 1 (over z), tp: 4 (over y), sp: 8 (over x, core).
Axes of the slice: x: 4, y: 4, z: 1, core: 2. Of those that a mesh axis runs over, the one named last changes fastest.
The devices are a block of a 4x4x8 slice.
Arguments:
- hidden: bfloat16 [1024, 4096], P('dp')
- start_pos: int32 [1], P('dp')
- k_cache: bfloat16 [16384, 8, 128], P(('dp', 'sp'), 'tp')
- v_cache: bfloat16 [16384, 8, 128], P(('dp', 'sp'), 'tp')
- norm_gain: float32 [4096], replicated
- w_query: bfloat16 [4096, 4096], P(None, 'tp')
- w_key: bfloat16 [4096, 1024], P(None, 'tp')
- w_value: bfloat16 [4096, 1024], P(None, 'tp')
- q_gain: float32 [128], replicated
- k_gain: float32 [128], replicated
- w_out: bfloat16 [4096, 4096], P('tp')
Outputs:
- output 1: bfloat16 [1024, 4096], P('dp')
- output 2: bfloat16 [16384, 8, 128], P(('dp', 'sp'), 'tp')
- output 3: bfloat16 [16384, 8, 128], P(('dp', 'sp'), 'tp')
All inputs are finite; a program needn't handle non-finite values.
Results may differ from a plain program's by a relative error of at most 0.00426084.
Values sent between devices are 32-bit elements.
A program may use at most 768 MiB of HBM per device.

v0:
```python
import functools
import math

import jax
import jax.numpy as jnp
from jax import lax
from jax.experimental import pallas as pl
from jax.experimental.pallas import tpu as pltpu
from jax.sharding import PartitionSpec as P

ROPE_BASE = 1e6
NORM_EPS = 1e-6
LANES = 128
STAGES = 4
STEP_AT = (
    (5, 10, 15, 20), (6, 11, 16, 21), (8, 13, 18, 22), (10, 15, 20, 24), (11, 16, 22, 27), (12, 18, 23, 28),
    (14, 20, 25, 29), (16, 22, 28, 31), (18, 24, 29, 32), (19, 26, 30, 33), (20, 27, 31, 34),
)
F32 = jnp.float32
BF16 = jnp.bfloat16
MESH = pl.DeviceIdType.MESH


def rms_norm(values, gain):
    mean_sq = jnp.mean(values * values, axis=-1, keepdims=True)
    return values * lax.rsqrt(mean_sq + NORM_EPS) * gain


def rope_tables(positions, head_dim):
    half_dim = head_dim // 2
    inv_freq = ROPE_BASE ** (-2.0 * jnp.arange(half_dim, dtype=F32) / head_dim)
    angles = positions.astype(F32)[:, None] * inv_freq[None, :]
    cosine, sine = jnp.cos(angles), jnp.sin(angles)
    return jnp.concatenate([cosine, cosine], axis=-1), jnp.concatenate([-sine, sine], axis=-1)


def merge(a, b, heads):
    d = (a.shape[1] - LANES) // heads
    sa, sb = a[:, heads * d:], b[:, heads * d:]
    top = jnp.maximum(sa, sb)
    ea, eb = jnp.exp2(sa - top), jnp.exp2(sb - top)
    lane = lax.broadcasted_iota(jnp.int32, sa.shape, 1)
    stats = jnp.where(lane < heads, top, sa * pltpu.roll(ea, heads, 1) + sb * pltpu.roll(eb, heads, 1))
    cols = [a[:, i * d:(i + 1) * d] * ea[:, i:i + 1] + b[:, i * d:(i + 1) * d] * eb[:, i:i + 1] for i in range(heads)]
    return jnp.concatenate(cols + [stats], axis=1)


def group_kernel(n_last, nx, ny, at_ref, h_hbm, wq_hbm, wk_hbm, wv_hbm, gain_ref, qg_ref, kg_ref, cos_hbm, sin_hbm, k_hbm, v_hbm, wout_hbm,
                 out_hbm, kn_hbm, vn_hbm,
                 wq, wk, wv, wout, h_buf, x_buf, cos_buf, sin_buf, k_buf, v_buf, q_buf, s0_buf, s1_buf, p0_buf, p1_buf, bias_old, bias_new, new_f32, k_rows, v_rows,
                 msg, chip, relay_x, final_x, part, relay_y, final_y, hrow, land, outb,
                 load_sem, table_sem, h_sem, hrow_sem, rows_sem, send_sem, recv_sem, piece_sem, share_sem, share_send, out_sem):
    stages, plane, width = chip.shape
    srows = 2 * plane
    model = wout.shape[1]
    half_model = model // 2
    xr_rows = plane // nx
    xh = xr_rows // 2
    yrows = xr_rows // ny
    sp = lax.axis_index("sp")
    y = lax.axis_index("tp")
    x, c = sp // 2, sp % 2
    oc = 1 - c
    x_r, x_l, x_o = (x + 1) % nx, (x + nx - 1) % nx, (x + 2) % nx
    y_r, y_l, y_o = (y + 1) % ny, (y + ny - 1) % ny, (y + 2) % ny
    partner = {"sp": x * 2 + oc}
    right, left = {"sp": x_r * 2 + c}, {"sp": x_l * 2 + c}
    up, down = {"tp": y_r}, {"tp": y_l}
    u = x * oc + y * c
    v = y * oc + x * c

    def axis_dev(d_first, d_second):
        return {"sp": ((x + oc * d_first + c * d_second + nx) % nx) * 2 + c, "tp": (y + c * d_first + oc * d_second + ny) % ny}

    u_r, u_l, v_r, v_l = axis_dev(1, 0), axis_dev(-1, 0), axis_dev(0, 1), axis_dev(0, -1)

    def piece_rows(du, dv):
        uu, vv = (u + du) % nx, (v + dv) % ny
        px, py = uu * oc + vv * c, vv * oc + uu * c
        return pl.multiple_of(c * plane + px * xr_rows + py * yrows, yrows)

    kv_heads, shard_len, head_dim = k_buf.shape
    heads = wq.shape[1] // head_dim
    group = heads // kv_heads
    old = shard_len - stages * srows
    pairs = heads // 2
    parts = 1 + pairs
    is_last = sp == n_last
    scale = head_dim ** -0.5 * math.log2(math.e)

    def ds(start, size):
        return pl.ds(pl.multiple_of(start, size), size)

    def h_load(b):
        return pltpu.make_async_copy(h_hbm.at[ds(b * srows, srows)], h_buf, h_sem.at[b])

    own_off = c * plane + x * xr_rows + y * yrows

    def hrow_load(b):
        return pltpu.make_async_copy(h_hbm.at[ds(b * srows + own_off, yrows)], hrow.at[b], hrow_sem.at[b])

    loads = [
        pltpu.make_async_copy(src, dst, load_sem.at[i])
        for i, (src, dst) in enumerate(((wq_hbm, wq), (k_hbm, k_buf), (v_hbm, v_buf), (wout_hbm, wout), (wk_hbm, wk), (wv_hbm, wv)))
    ]

    def table_load(b, i):
        src, dst = ((cos_hbm, cos_buf), (sin_hbm, sin_buf))[i]
        return pltpu.make_async_copy(src.at[ds(b * srows, srows)], dst.at[b % 2], table_sem.at[b, i])

    h_load(0).start()
    for i in range(2):
        table_load(0, i).start()
    for i in range(3):
        loads[i].start()

    @pl.when(is_last)
    def _():
        loads[4].start()
        loads[5].start()

    loads[3].start()
    for b in range(stages):
        hrow_load(b).start()

    barrier = pltpu.get_barrier_semaphore()
    for dev in (partner, right, left, up, down):
        pl.semaphore_signal(barrier, inc=1, device_id=dev, device_id_type=MESH)
    pl.semaphore_wait(barrier, 5)

    def copy(src, dst, ssem, rsem, dev):
        return pltpu.make_async_remote_copy(src_ref=src, dst_ref=dst, send_sem=ssem, recv_sem=rsem, device_id=dev, device_id_type=MESH)

    def m_share(b):
        return copy(msg.at[b % 2, ds(oc * plane, plane)], chip.at[b], send_sem.at[b, 0], recv_sem.at[b, 0], partner)

    def m_x(b, i):
        src, dst, dev = [
            (ds(x_o * xr_rows, xh), relay_x.at[b, 0], right),
            (ds(x_o * xr_rows + xh, xh), relay_x.at[b, 1], left),
            (ds(x_r * xr_rows + xh, xh), final_x.at[b, 0, pl.ds(xh, xh)], right),
            (ds(x_l * xr_rows, xh), final_x.at[b, 1, pl.ds(0, xh)], left),
            (ds(x_r * xr_rows, xh), final_x.at[b, 0, pl.ds(0, xh)], right),
            (ds(x_l * xr_rows + xh, xh), final_x.at[b, 1, pl.ds(xh, xh)], left),
        ][i]
        return copy(chip.at[b, src], dst, send_sem.at[b, 1 + i], recv_sem.at[b, 1 + i], dev)

    lo, hi = pl.ds(0, half_model), pl.ds(half_model, half_model)

    def m_y(b, i):
        src, dst, dev = [
            (part.at[b, ds(y_o * yrows, yrows), lo], relay_y.at[b, 0], up),
            (part.at[b, ds(y_o * yrows, yrows), hi], relay_y.at[b, 1], down),
            (part.at[b, ds(y_r * yrows, yrows), hi], final_y.at[b, 0, :, hi], up),
            (part.at[b, ds(y_l * yrows, yrows), lo], final_y.at[b, 1, :, lo], down),
            (part.at[b, ds(y_r * yrows, yrows), lo], final_y.at[b, 0, :, lo], up),
            (part.at[b, ds(y_l * yrows, yrows), hi], final_y.at[b, 1, :, hi], down),
        ][i]
        return copy(src, dst, send_sem.at[b, 7 + i], recv_sem.at[b, 7 + i], dev)

    def piece(b, du, dv, half):
        rows = pl.ds(piece_rows(du, dv), yrows)
        return land.at[b, rows] if half is None else land.at[b, rows, lo if half == 0 else hi]

    def sem_of(du, dv, half):
        return ((du % 4) * 4 + dv % 4) * 2 + (half or 0)

    def g_first(b, to, du, half):
        ref = piece(b, du, 0, half)
        s = sem_of(du - to, 0, half)
        return copy(ref, ref, send_sem.at[b, 13 + (0 if to == 1 else 1) + (2 if half is not None else 0)], piece_sem.at[b, s], u_r if to == 1 else u_l)

    def g_second(b, to, du, dv, half):
        ref = piece(b, du, dv, half)
        s = sem_of(du, dv - to, half)
        return copy(ref, ref, send_sem.at[b, 17 + (du % 4) * 4 + (0 if to == 1 else 1) + (2 if dv else 0)], piece_sem.at[b, s], v_r if to == 1 else v_l)

    def g_share(b, du, dv):
        ref = piece(b, du, dv, None)
        k = (du % 4) * 4 + dv % 4
        return copy(ref, ref, share_send.at[b, k], share_sem.at[b, k], partner)

    def wait_piece(b, du, dv, half):
        ref = piece(b, du, dv, half)
        copy(ref, ref, send_sem.at[b, 0], piece_sem.at[b, sem_of(du, dv, half)], partner).wait_recv()

    def wait_share(b, k):
        uu, vv = (x * c + y * oc + k // 4) % nx, (y * c + x * oc + k % 4) % nx
        row = oc * plane + (uu * c + vv * oc) * xr_rows + (vv * c + uu * oc) * yrows
        ref = land.at[b, pl.ds(pl.multiple_of(row, yrows), yrows)]
        copy(ref, ref, share_send.at[b, k], share_sem.at[b, k], partner).wait_recv()

    def s0(b):
        m_share(b).start()

    def s1(b):
        m_share(b).wait_recv()
        chip[b] = merge(chip[b], msg[b % 2, ds(c * plane, plane)], heads)
        for i in range(4):
            m_x(b, i).start()

    def s2(b):
        for i, dest in ((0, x_r * xr_rows), (1, x_l * xr_rows + xh)):
            m_x(b, i).wait_recv()
            rows = ds(dest, xh)
            chip[b, rows] = merge(chip[b, rows], relay_x[b, i], heads)
            m_x(b, 4 + i).start()

    def s3(b):
        @pl.when(b == 0)
        def _():
            loads[3].wait()

        for i in range(2, 6):
            m_x(b, i).wait_recv()
        total = merge(chip[b, ds(x * xr_rows, xr_rows)], final_x[b, 0], heads)
        total = merge(total, final_x[b, 1], heads)
        d = (width - LANES) // heads
        base = heads * d + heads
        att = jnp.concatenate([(total[:, i * d:(i + 1) * d] / total[:, base + i:base + i + 1]).astype(BF16) for i in range(heads)], axis=1)
        for j in range(4):
            cols = slice(j * (model // 4), (j + 1) * (model // 4))
            part[b, :, cols] = jnp.dot(att, wout[:, cols], preferred_element_type=F32)
        for i in range(4):
            m_y(b, i).start()

    def s4(b):
        for i, (dest, cols) in enumerate(((y_r, lo), (y_l, hi))):
            m_y(b, i).wait_recv()
            rows = ds(dest * yrows, yrows)
            part[b, rows, cols] = part[b, rows, cols] + relay_y[b, i]
            m_y(b, 4 + i).start()

    def s5(b):
        for i in range(2, 6):
            m_y(b, i).wait_recv()
        hrow_load(b).wait()
        total = part[b, ds(y * yrows, yrows)] + final_y[b, 0] + final_y[b, 1]
        land[b, pl.ds(piece_rows(0, 0), yrows)] = total + hrow[b].astype(F32)
        g_first(b, 1, 0, None).start()
        g_first(b, -1, 0, None).start()
        g_second(b, 1, 0, 0, None).start()
        g_second(b, -1, 0, 0, None).start()
        g_share(b, 0, 0).start()

    def arrive_second(b, du):
        wait_piece(b, du, -1, None)
        g_second(b, 1, du, -1, 0).start()
        wait_piece(b, du, 1, None)
        g_second(b, -1, du, 1, 1).start()
        g_share(b, du, -1).start()
        g_share(b, du, 1).start()

    def arrive_far(b, du):
        for half in range(2):
            wait_piece(b, du, 2, half)
        g_share(b, du, 2).start()

    def s6(b):
        wait_piece(b, -1, 0, None)
        g_first(b, 1, -1, 0).start()
        wait_piece(b, 1, 0, None)
        g_first(b, -1, 1, 1).start()
        for du in (-1, 1):
            g_second(b, 1, du, 0, None).start()
            g_second(b, -1, du, 0, None).start()
            g_share(b, du, 0).start()
        arrive_second(b, 0)

    def s7(b):
        wait_piece(b, 2, 0, 0)
        wait_piece(b, 2, 0, 1)
        g_second(b, 1, 2, 0, None).start()
        g_second(b, -1, 2, 0, None).start()
        g_share(b, 2, 0).start()
        arrive_second(b, -1)
        arrive_second(b, 1)
        arrive_far(b, 0)

    def s8(b):
        arrive_second(b, 2)
        arrive_far(b, -1)
        arrive_far(b, 1)

    def s9(b):
        arrive_far(b, 2)

    def out_copy(b):
        return pltpu.make_async_copy(outb, out_hbm.at[pl.ds(pl.multiple_of(b * srows, srows), srows)], out_sem.at[b])

    def s10(b):
        for k in range(16):
            wait_share(b, k)

        @pl.when(b > 0)
        def _():
            out_copy(b - 1).wait()

        @pl.loop(0, srows // 16)
        def _(r):
            rows = pl.ds(pl.multiple_of(r * 16, 16), 16)
            outb[rows] = land[b, rows].astype(BF16)
        out_copy(b).start()

    lane = lax.broadcasted_iota(jnp.int32, (srows, LANES), 1)
    s_bufs, p_bufs = (s0_buf, s1_buf), (p0_buf, p1_buf)

    def kv_rows_copy(b, i):
        src, dst = ((k_rows, kn_hbm), (v_rows, vn_hbm))[i]
        return pltpu.make_async_copy(src, dst.at[ds(b * srows, srows)], rows_sem.at[b, i])

    def scores(head, slot, kb):
        q, k = q_buf[head], head // group
        nt = (((1,), (1,)), ((), ()))
        if kb is None:
            s_bufs[slot][...] = lax.dot_general(q, k_buf[k], nt, preferred_element_type=F32)
            return
        seen = old + kb * srows
        s_bufs[slot][:, :old] = lax.dot_general(q, k_buf[k, :old], nt, preferred_element_type=F32) + bias_old[...]
        if kb:
            s_bufs[slot][:, old:seen] = lax.dot_general(q, k_buf[k, old:seen], nt, preferred_element_type=F32)
        s_bufs[slot][:, seen:seen + srows] = lax.dot_general(q, k_buf[k, seen:seen + srows], nt, preferred_element_type=F32) + bias_new[...]

    def one_head(b, head, slot, kb, stats):
        keys = shard_len if kb is None else old + (kb + 1) * srows
        s = s_bufs[slot][:, :keys]
        m = jnp.max(s, axis=-1, keepdims=True)
        w = jnp.exp2((s - m) * scale)
        total = jnp.sum(w, axis=-1, keepdims=True)
        p_bufs[slot][:, :keys] = w.astype(BF16)
        num = jnp.dot(p_bufs[slot][:, :keys], v_buf[head // group, :keys], preferred_element_type=F32)
        msg[b % 2, :, pl.ds(pl.multiple_of(head * head_dim, head_dim), head_dim)] = num
        return jnp.where(lane == head, m * scale, jnp.where(lane == heads + head, total, stats))

    def each_variant(b, fn):
        @pl.when(jnp.logical_not(is_last))
        def _():
            fn(None)

        for kb in range(stages):
            @pl.when(jnp.logical_and(is_last, b == kb))
            def _():
                fn(kb)

    def project(b):
        @pl.when(b >= 2)
        def _():
            m_share(b - 2).wait_send()

        h_load(b).wait()

        @pl.loop(0, srows // 16, unroll=2)
        def _(r):
            rows = ds(r * 16, 16)
            hf = h_buf[rows].astype(F32)
            mean_sq = jnp.mean(hf * hf, axis=-1, keepdims=True)
            x_buf[rows] = (hf * lax.rsqrt(mean_sq + NORM_EPS) * gain_ref[...]).astype(BF16)

        @pl.when(b + 1 < stages)
        def _():
            h_load(b + 1).start()
            table_load(b + 1, 0).start()
            table_load(b + 1, 1).start()

        @pl.when(b == 0)
        def _():
            for i in range(3):
                loads[i].wait()

        table_load(b, 0).wait()
        table_load(b, 1).wait()

        def rope(one):
            return one * cos_buf[b % 2] + pltpu.roll(one, head_dim // 2, 1) * sin_buf[b % 2]

        def project_pair(pair, carry):
            proj = jnp.dot(x_buf[...], wq[:, ds(pair * 2 * head_dim, 2 * head_dim)], preferred_element_type=F32)
            for j in range(2):
                q_buf[pair * 2 + j] = rope(rms_norm(proj[:, j * head_dim:(j + 1) * head_dim], qg_ref[...])).astype(BF16)
            return carry

        lax.fori_loop(0, pairs, project_pair, 0)

        @pl.when(is_last)
        def _():
            @pl.when(b == 0)
            def _():
                loads[4].wait()
                loads[5].wait()
                key = lax.broadcasted_iota(jnp.int32, bias_old.shape, 1)
                bias_old[...] = jnp.where(key < at_ref[0], 0.0, -jnp.inf)
                row = lax.broadcasted_iota(jnp.int32, bias_new.shape, 0)
                col = lax.broadcasted_iota(jnp.int32, bias_new.shape, 1)
                bias_new[...] = jnp.where(col <= row, 0.0, -jnp.inf)

            @pl.when(b > 0)
            def _():
                kv_rows_copy(b - 1, 0).wait()
                kv_rows_copy(b - 1, 1).wait()

            new = ds(old + b * srows, srows)
            proj = jnp.dot(x_buf[...], wk[...], preferred_element_type=F32)
            for j in range(kv_heads):
                one = rope(rms_norm(proj[:, j * head_dim:(j + 1) * head_dim], kg_ref[...]))
                k_buf[j, new] = one.astype(BF16)
                new_f32[:, j, :] = one
            k_rows[...] = new_f32[...].astype(BF16)
            proj = jnp.dot(x_buf[...], wv[...], preferred_element_type=F32)
            for j in range(kv_heads):
                one = proj[:, j * head_dim:(j + 1) * head_dim]
                v_buf[j, new] = one.astype(BF16)
                new_f32[:, j, :] = one
            v_rows[...] = new_f32[...].astype(BF16)
            kv_rows_copy(b, 0).start()
            kv_rows_copy(b, 1).start()

        msg[b % 2, :, heads * head_dim:] = jnp.zeros((srows, LANES), F32)
        each_variant(b, lambda kb: scores(0, 0, kb))

    def attend_pair(b, j):
        def run(kb):
            stats = msg[b % 2, :, heads * head_dim:]
            scores(2 * j + 1, 1, kb)
            stats = one_head(b, 2 * j, 0, kb, stats)
            scores(jnp.minimum(2 * j + 2, heads - 1), 0, kb)
            msg[b % 2, :, heads * head_dim:] = one_head(b, 2 * j + 1, 1, kb, stats)

        each_variant(b, run)

    steps = [s0, s1, s2, s3, s4, s5, s6, s7, s8, s9, s10]

    @pl.loop(0, max(STEP_AT[-1]) + 1)
    def _(t):
        for k in reversed(range(len(steps))):
            due, passed = t == STEP_AT[k][0], 0
            for at in STEP_AT[k][1:]:
                due = jnp.logical_or(due, t == at)
                passed = passed + (t >= at).astype(jnp.int32)

            @pl.when(due)
            def _():
                steps[k](passed)

        b = t // parts

        @pl.when(jnp.logical_and(b < stages, t % parts == 0))
        def _():
            project(b)

        @pl.when(jnp.logical_and(b < stages, t % parts > 0))
        def _():
            attend_pair(b, t % parts - 1)

    @pl.when(is_last)
    def _():
        kv_rows_copy(stages - 1, 0).wait()
        kv_rows_copy(stages - 1, 1).wait()

    out_copy(stages - 1).wait()
    for b in range(stages):
        if b >= stages - 2:
            m_share(b).wait_send()
        for i in range(6):
            m_x(b, i).wait_send()
            m_y(b, i).wait_send()
        for to in (1, -1):
            g_first(b, to, 0, None).wait_send()
            g_first(b, to, -to, 0 if to == 1 else 1).wait_send()
            for du in range(4):
                g_second(b, to, du, 0, None).wait_send()
                g_second(b, to, du, -to, 0 if to == 1 else 1).wait_send()
        for du in range(4):
            for dv in range(4):
                g_share(b, du, dv).wait_send()


def attend_and_combine(mesh, write_at, hidden, w_query, w_key, w_value, norm_gain, q_gain, k_gain, cosine, sine, k_heads, v_heads, w_out):
    chunk, model = hidden.shape
    kv_heads, shard_len, head_dim = k_heads.shape
    width = w_query.shape[1] + LANES
    kv_width = w_key.shape[1]
    nx, ny = mesh.shape["sp"] // 2, mesh.shape["tp"]
    assert nx == 4 and ny == 4
    srows = chunk // STAGES
    plane = srows // 2
    xr_rows = plane // nx
    yrows = xr_rows // ny
    dma = pltpu.SemaphoreType.DMA
    anywhere = pl.BlockSpec(memory_space=pl.ANY)
    vmem = pl.BlockSpec(memory_space=pltpu.VMEM)
    new_rows = jax.ShapeDtypeStruct((chunk, kv_heads, head_dim), BF16)
    return pl.pallas_call(
        functools.partial(group_kernel, mesh.shape["sp"] - 1, nx, ny),
        name="attend_and_combine",
        out_shape=(jax.ShapeDtypeStruct((chunk, model), BF16), new_rows, new_rows),
        in_specs=[pl.BlockSpec(memory_space=pltpu.SMEM)] + [anywhere] * 4 + [vmem] * 3 + [anywhere] * 5,
        out_specs=(anywhere,) * 3,
        scratch_shapes=[
            pltpu.VMEM(w_query.shape, BF16),
            pltpu.VMEM(w_key.shape, BF16),
            pltpu.VMEM(w_value.shape, BF16),
            pltpu.VMEM(w_out.shape, BF16),
            pltpu.VMEM((srows, model), BF16),
            pltpu.VMEM((srows, model), BF16),
            pltpu.VMEM((2, srows, head_dim), F32),
            pltpu.VMEM((2, srows, head_dim), F32),
            pltpu.VMEM(k_heads.shape, BF16),
            pltpu.VMEM(v_heads.shape, BF16),
            pltpu.VMEM((w_query.shape[1] // head_dim, srows, head_dim), BF16),
            pltpu.VMEM((srows, shard_len), F32),
            pltpu.VMEM((srows, shard_len), F32),
            pltpu.VMEM((srows, shard_len), BF16),
            pltpu.VMEM((srows, shard_len), BF16),
            pltpu.VMEM((1, shard_len - chunk), F32),
            pltpu.VMEM((srows, srows), F32),
            pltpu.VMEM((srows, kv_heads, head_dim), F32),
            pltpu.VMEM((srows, kv_heads, head_dim), BF16),
            pltpu.VMEM((srows, kv_heads, head_dim), BF16),
            pltpu.VMEM((2, srows, width), F32),
            pltpu.VMEM((STAGES, plane, width), F32),
            pltpu.VMEM((STAGES, 2, xr_rows // 2, width), F32),
            pltpu.VMEM((STAGES, 2, xr_rows, width), F32),
            pltpu.VMEM((STAGES, xr_rows, model), F32),
            pltpu.VMEM((STAGES, 2, yrows, model // 2), F32),
            pltpu.VMEM((STAGES, 2, yrows, model), F32),
            pltpu.VMEM((STAGES, yrows, model), BF16),
            pltpu.VMEM((STAGES, srows, model), F32),
            pltpu.VMEM((srows, model), BF16),
            dma((6,)),
            dma((STAGES, 2)),
            dma((STAGES,)),
            dma((STAGES,)),
            dma((STAGES, 2)),
            dma((STAGES, 33)),
            dma((STAGES, 13)),
            dma((STAGES, 32)),
            dma((STAGES, 16)),
            dma((STAGES, 16)),
            dma((STAGES,)),
        ],
        compiler_params=pltpu.CompilerParams(collective_id=0, has_side_effects=True, vmem_limit_bytes=67043328),
    )(write_at.reshape(1), hidden, w_query, w_key, w_value, norm_gain.reshape(1, model), q_gain.reshape(1, head_dim), k_gain.reshape(1, head_dim),
      cosine, sine, k_heads, v_heads, w_out)


def finish_kernel(n_last, pieces, at_ref, out_in, k_in, v_in, kn_in, vn_in, out_ref, k_out, v_out, out_buf, k_buf, v_buf, kn_buf, vn_buf, sem):
    is_last = lax.axis_index("sp") == n_last
    rows = out_in.shape[0] // pieces
    reads = [pltpu.make_async_copy(k_in, k_buf, sem.at[0, 0]), pltpu.make_async_copy(v_in, v_buf, sem.at[0, 1])]
    writes = [pltpu.make_async_copy(k_buf, k_out, sem.at[1, 0]), pltpu.make_async_copy(v_buf, v_out, sem.at[1, 1])]
    for i in range(pieces):
        here = pl.ds(i * rows, rows)
        reads.append(pltpu.make_async_copy(out_in.at[here], out_buf.at[here], sem.at[0, 2 + i]))
        writes.append(pltpu.make_async_copy(out_buf.at[here], out_ref.at[here], sem.at[1, 2 + i]))
    where = pl.ds(at_ref[0], kn_buf.shape[0])
    new_reads = [pltpu.make_async_copy(src, dst, sem.at[0, 2 + pieces + i]) for i, (src, dst) in enumerate(((kn_in, kn_buf), (vn_in, vn_buf)))]
    new_writes = [pltpu.make_async_copy(src, dst.at[where], sem.at[1, 2 + pieces + i]) for i, (src, dst) in enumerate(((kn_buf, k_out), (vn_buf, v_out)))]
    for read in reads:
        read.start()

    @pl.when(is_last)
    def _():
        for read in new_reads:
            read.start()

    for read, write in zip(reads, writes):
        read.wait()
        write.start()
    for write in writes[:2]:
        write.wait()

    @pl.when(is_last)
    def _():
        for read, write in zip(new_reads, new_writes):
            read.wait()
            write.start()
        for write in new_writes:
            write.wait()

    for write in writes[2:]:
        write.wait()


def finish(n_last, write_at, out, k_shard, v_shard, k_new, v_new):
    pieces = 8
    anywhere = pl.BlockSpec(memory_space=pl.ANY)
    return pl.pallas_call(
        functools.partial(finish_kernel, n_last, pieces),
        name="finish",
        out_shape=tuple(jax.ShapeDtypeStruct(a.shape, a.dtype) for a in (out, k_shard, v_shard)),
        in_specs=[pl.BlockSpec(memory_space=pltpu.SMEM)] + [anywhere] * 5,
        out_specs=(anywhere,) * 3,
        scratch_shapes=[pltpu.VMEM(a.shape, a.dtype) for a in (out, k_shard, v_shard, k_new, v_new)] + [pltpu.SemaphoreType.DMA((2, pieces + 4))],
        compiler_params=pltpu.CompilerParams(vmem_limit_bytes=67043328),
    )(write_at.reshape(1), out, k_shard, v_shard, k_new, v_new)


def solution(mesh):
    cache_spec = P(("dp", "sp"), "tp", None)
    in_specs = (P("dp", None), P("dp"), cache_spec, cache_spec, P(None), P(None, "tp"), P(None, "tp"), P(None, "tp"), P(None), P(None), P("tp", None))
    out_specs = (P("dp", None), cache_spec, cache_spec)
    n_last = mesh.shape["sp"] - 1

    def local_step(hidden, start_pos, k_shard, v_shard, norm_gain, w_query, w_key, w_value, q_gain, k_gain, w_out):
        chunk_len, model_dim = hidden.shape
        shard_len, kv_local, head_dim = k_shard.shape
        first_pos = start_pos[0]
        cosine, sine = rope_tables(first_pos + jnp.arange(chunk_len, dtype=jnp.int32), head_dim)

        write_at = first_pos - n_last * shard_len
        k_heads, v_heads = jnp.transpose(k_shard, (1, 0, 2)), jnp.transpose(v_shard, (1, 0, 2))
        out, k_new, v_new = attend_and_combine(mesh, write_at, hidden, w_query, w_key, w_value, norm_gain, q_gain, k_gain, cosine, sine, k_heads, v_heads, w_out)
        return finish(n_last, write_at, out, k_shard, v_shard, k_new, v_new)

    return jax.shard_map(local_step, mesh=mesh, in_specs=in_specs, out_specs=out_specs, check_vma=False)
```

profile of v0, /device:TPU:97, one launch (start us, length us, event | category | flops | bytes accessed | tf_op | source)
XLA Modules:
  0.0 146.8 jit_solution(15515828804384774067)
XLA Ops:
  1.3 1.9 %fusion = (f32[1024,64]{1,0:T(8,128)S(1)}, f32[1024,64]{1,0:T(8,128)S(1)}, f32[1024,64]{1,0:T(8,128)S(1)}) fusion(f32[64]{0:T(128)S(1)} %multiply_power_fusion, f32[1024]{0:T(1024)S(1)} %add_convert_fusion), kind=kLoop, calls=%fused_computation.6 | loop fusion | flops 131072 | bytes 790784 | tf_op jit(solution)/shard_map/neg | solution.py:34
  3.2 1.3 pad_maximum_fusion
  4.5 3.1 %copy_bitcast_fusion = (bf16[2,2048,128]{2,1,0:T(8,128)(2,1)}, bf16[2,2048,128]{2,1,0:T(8,128)(2,1)}) fusion(bf16[2048,2,128]{2,1,0:T(2,128)(2,1)} %v_in.1, bf16[2048,2,128]{2,1,0:T(2,128)(2,1)} %k_in.1), kind=kLoop, calls=%fused_computation | loop fusion | bytes 4194304 | tf_op jit(solution)/shard_map/transpose | solution.py:611
  7.6 130.7 %attend_and_combine.1 = (bf16[1024,4096]{1,0:T(8,128)(2,1)}, bf16[1024,2,128]{2,1,0:T(2,128)(2,1)}, bf16[1024,2,128]{2,1,0:T(2,128)(2,1)}) custom-call(s32[1]{0:T(128)} %bitcast.1.at_ref, bf16[1024,4096]{1,0:T(8,128)(2,1)} %h_hbm.1, bf16[4096,1024]{1,0:T(8,128)(2,1)} %wq_hbm.1, bf16[4096,256]{1,0:T(8,128)(2,1)} %wk_hbm.1, bf16[4096,256]{1,0:T(8,128)(2,1)} %wv_hbm.1, ...), custom_call_target="tpu_custom_call" | custom-call | tf_op jit(solution)/shard_map/attend_and_combine/pallas_call | solution.py:492
  138.4 8.2 %finish.1 = (bf16[1024,4096]{1,0:T(8,128)(2,1)}, bf16[2048,2,128]{2,1,0:T(2,128)(2,1)}, bf16[2048,2,128]{2,1,0:T(2,128)(2,1)}) custom-call(s32[1]{0:T(128)} %bitcast.1.at_ref, bf16[1024,4096]{1,0:T(8,128)(2,1)} %get-tuple-element.6.out_in, bf16[2048,2,128]{2,1,0:T(2,128)(2,1)} %k_in.1, bf16[2048,2,128]{2,1,0:T(2,128)(2,1)} %v_in.1, ...), custom_call_target="tpu_custom_call" | custom-call | tf_op jit(solution)/shard_map/finish/pallas_call | solution.py:587
  (2 shorter events, 0.0 us)
where the time goes:
time: 147 us
  Pallas kernels  139 us (95%)
  other arithmetic  3.21 us (2%)
  local copies, waits for them, and re-layouts  3.13 us (2%)
    pallas_call x1, Pallas kernels, attend_and_combine(): pl.pallas_call(functools.partial(group_kernel, mesh.shape['sp'] - 1, nx,...  131 us
    pallas_call x1, Pallas kernels, finish(): pl.pallas_call(functools.partial(finish_kernel, n_last, pieces), name='fi...  8.23 us
    transpose x1, local copies, waits for them, and re-layouts, local_step(): jnp.transpose(v_shard, (1, 0, 2))  3.13 us

commit v1 on v0

--- a/solution.py
+++ b/solution.py
@@ -13,8 +13,9 @@
 LANES = 128
 STAGES = 4
 STEP_AT = (
-    (5, 10, 15, 20), (6, 11, 16, 21), (8, 13, 18, 22), (10, 15, 20, 24), (11, 16, 22, 27), (12, 18, 23, 28),
-    (14, 20, 25, 29), (16, 22, 28, 31), (18, 24, 29, 32), (19, 26, 30, 33), (20, 27, 31, 34),
+    (5, 10, 15, 20), (6, 11, 16, 21), (9, 13, 20, 22), (11, 15, 22, 25),
+    (13, 16, 24, 27), (15, 20, 26, 29), (16, 22, 28, 30), (19, 25, 30, 31),
+    (22, 27, 31, 33), (23, 29, 32, 34), (24, 30, 33, 35),
 )
 F32 = jnp.float32
 BF16 = jnp.bfloat16
@@ -31,7 +32,7 @@
     inv_freq = ROPE_BASE ** (-2.0 * jnp.arange(half_dim, dtype=F32) / head_dim)
     angles = positions.astype(F32)[:, None] * inv_freq[None, :]
     cosine, sine = jnp.cos(angles), jnp.sin(angles)
-    return jnp.concatenate([cosine, cosine], axis=-1), jnp.concatenate([-sine, sine], axis=-1)
+    return cosine, sine
 
 
 def merge(a, b, heads):
@@ -47,9 +48,9 @@
 
 def group_kernel(n_last, nx, ny, at_ref, h_hbm, wq_hbm, wk_hbm, wv_hbm, gain_ref, qg_ref, kg_ref, cos_hbm, sin_hbm, k_hbm, v_hbm, wout_hbm,
                  out_hbm, kn_hbm, vn_hbm,
-                 wq, wk, wv, wout, h_buf, x_buf, cos_buf, sin_buf, k_buf, v_buf, q_buf, s0_buf, s1_buf, p0_buf, p1_buf, bias_old, bias_new, new_f32, k_rows, v_rows,
+                 wq, wk, wv, wout, h_buf, x_buf, cos_buf, sin_buf, k_buf, v_buf, q_buf, q_send, q_recv, s0_buf, s1_buf, p0_buf, p1_buf, bias_old, bias_new, new_f32, k_rows, v_rows,
                  msg, chip, relay_x, final_x, part, relay_y, final_y, hrow, land, outb,
-                 load_sem, table_sem, h_sem, hrow_sem, rows_sem, send_sem, recv_sem, piece_sem, share_sem, share_send, out_sem):
+                 load_sem, q_sem, table_sem, h_sem, hrow_sem, rows_sem, send_sem, recv_sem, piece_sem, share_sem, share_send, out_sem):
     stages, plane, width = chip.shape
     srows = 2 * plane
     model = wout.shape[1]
@@ -80,7 +81,9 @@
         return pl.multiple_of(c * plane + px * xr_rows + py * yrows, yrows)
 
     kv_heads, shard_len, head_dim = k_buf.shape
-    heads = wq.shape[1] // head_dim
+    own_width = wq.shape[1]
+    own_heads = own_width // head_dim
+    heads = 2 * own_heads
     group = heads // kv_heads
     old = shard_len - stages * srows
     pairs = heads // 2
@@ -91,6 +94,10 @@
     def ds(start, size):
         return pl.ds(pl.multiple_of(start, size), size)
 
+    def q_share(b):
+        return pltpu.make_async_remote_copy(
+            src_ref=q_send, dst_ref=q_recv.at[b % 2], send_sem=q_sem.at[0, b], recv_sem=q_sem.at[1, b], device_id=partner, device_id_type=MESH)
+
     def h_load(b):
         return pltpu.make_async_copy(h_hbm.at[ds(b * srows, srows)], h_buf, h_sem.at[b])
 
@@ -101,8 +108,9 @@
 
     loads = [
         pltpu.make_async_copy(src, dst, load_sem.at[i])
-        for i, (src, dst) in enumerate(((wq_hbm, wq), (k_hbm, k_buf), (v_hbm, v_buf), (wout_hbm, wout), (wk_hbm, wk), (wv_hbm, wv)))
+        for i, (src, dst) in enumerate(((k_hbm, k_buf), (v_hbm, v_buf), (wout_hbm, wout), (wk_hbm, wk), (wv_hbm, wv)))
     ]
+    loads.append(pltpu.make_async_copy(wq_hbm.at[:, ds(c * own_width, own_width)], wq, load_sem.at[5]))
 
     def table_load(b, i):
         src, dst = ((cos_hbm, cos_buf), (sin_hbm, sin_buf))[i]
@@ -111,15 +119,15 @@
     h_load(0).start()
     for i in range(2):
         table_load(0, i).start()
-    for i in range(3):
-        loads[i].start()
+    loads[5].start()
 
     @pl.when(is_last)
     def _():
+        loads[3].start()
         loads[4].start()
-        loads[5].start()
-
-    loads[3].start()
+
+    loads[0].start()
+    loads[1].start()
     for b in range(stages):
         hrow_load(b).start()
 
@@ -209,7 +217,7 @@
     def s3(b):
         @pl.when(b == 0)
         def _():
-            loads[3].wait()
+            loads[2].wait()
 
         for i in range(2, 6):
             m_x(b, i).wait_recv()
@@ -285,22 +293,44 @@
     def s9(b):
         arrive_far(b, 2)
 
-    def out_copy(b):
-        return pltpu.make_async_copy(outb, out_hbm.at[pl.ds(pl.multiple_of(b * srows, srows), srows)], out_sem.at[b])
+    def out_copy(b, core):
+        rows = ds(core * plane, plane)
+        return pltpu.make_async_copy(outb.at[rows], out_hbm.at[ds(b * srows + core * plane, plane)], out_sem.at[b, 0])
+
+    def out_copy_2(b, core):
+        rows = ds(core * plane, plane)
+        return pltpu.make_async_copy(outb.at[rows], out_hbm.at[ds(b * srows + core * plane, plane)], out_sem.at[b, 1])
+
+    def write_plane(b, core):
+        @pl.loop(0, plane // 16)
+        def _(r):
+            rows = ds(core * plane + r * 16, 16)
+            outb[rows] = land[b, rows].astype(BF16)
 
     def s10(b):
+        @pl.when(b > 0)
+        def _():
+            out_copy(b - 1, c).wait()
+            out_copy_2(b - 1, oc).wait()
+
+        write_plane(b, c)
+        out_copy(b, c).start()
+        for i in range(6):
+            m_x(b, i).wait_send()
+            m_y(b, i).wait_send()
+        for to in (1, -1):
+            g_first(b, to, 0, None).wait_send()
+            g_first(b, to, -to, 0 if to == 1 else 1).wait_send()
+            for du in range(4):
+                g_second(b, to, du, 0, None).wait_send()
+                g_second(b, to, du, -to, 0 if to == 1 else 1).wait_send()
+        for du in range(4):
+            for dv in range(4):
+                g_share(b, du, dv).wait_send()
         for k in range(16):
             wait_share(b, k)
-
-        @pl.when(b > 0)
-        def _():
-            out_copy(b - 1).wait()
-
-        @pl.loop(0, srows // 16)
-        def _(r):
-            rows = pl.ds(pl.multiple_of(r * 16, 16), 16)
-            outb[rows] = land[b, rows].astype(BF16)
-        out_copy(b).start()
+        write_plane(b, oc)
+        out_copy_2(b, oc).start()
 
     lane = lax.broadcasted_iota(jnp.int32, (srows, LANES), 1)
     s_bufs, p_bufs = (s0_buf, s1_buf), (p0_buf, p1_buf)
@@ -362,31 +392,43 @@
             table_load(b + 1, 0).start()
             table_load(b + 1, 1).start()
 
-        @pl.when(b == 0)
-        def _():
-            for i in range(3):
-                loads[i].wait()
-
         table_load(b, 0).wait()
         table_load(b, 1).wait()
 
+        cosine, sine = cos_buf[b % 2], sin_buf[b % 2]
+        cosine, sine = jnp.concatenate([cosine, cosine], axis=1), jnp.concatenate([-sine, sine], axis=1)
+
         def rope(one):
-            return one * cos_buf[b % 2] + pltpu.roll(one, head_dim // 2, 1) * sin_buf[b % 2]
-
-        def project_pair(pair, carry):
-            proj = jnp.dot(x_buf[...], wq[:, ds(pair * 2 * head_dim, 2 * head_dim)], preferred_element_type=F32)
+            return one * cosine + pltpu.roll(one, head_dim // 2, 1) * sine
+
+        @pl.when(b == 0)
+        def _():
+            loads[5].wait()
+
+        @pl.when(b > 0)
+        def _():
+            q_share(b - 1).wait_send()
+
+        for pair in range(own_heads // 2):
+            proj = jnp.dot(x_buf[...], wq[:, pair * 2 * head_dim:(pair + 1) * 2 * head_dim], preferred_element_type=F32)
             for j in range(2):
-                q_buf[pair * 2 + j] = rope(rms_norm(proj[:, j * head_dim:(j + 1) * head_dim], qg_ref[...])).astype(BF16)
-            return carry
-
-        lax.fori_loop(0, pairs, project_pair, 0)
+                one = rope(rms_norm(proj[:, j * head_dim:(j + 1) * head_dim], qg_ref[...]))
+                q_send[pair * 2 + j] = one
+                q_buf[c * own_heads + pair * 2 + j] = one.astype(BF16)
+        q_share(b).start()
+
+        @pl.when(b == 0)
+        def _():
+            loads[2].start()
+            loads[0].wait()
+            loads[1].wait()
 
         @pl.when(is_last)
         def _():
             @pl.when(b == 0)
             def _():
+                loads[3].wait()
                 loads[4].wait()
-                loads[5].wait()
                 key = lax.broadcasted_iota(jnp.int32, bias_old.shape, 1)
                 bias_old[...] = jnp.where(key < at_ref[0], 0.0, -jnp.inf)
                 row = lax.broadcasted_iota(jnp.int32, bias_new.shape, 0)
@@ -415,15 +457,24 @@
             kv_rows_copy(b, 1).start()
 
         msg[b % 2, :, heads * head_dim:] = jnp.zeros((srows, LANES), F32)
-        each_variant(b, lambda kb: scores(0, 0, kb))
+        each_variant(b, lambda kb: scores(c * own_heads, 0, kb))
 
     def attend_pair(b, j):
+        @pl.when(j == pairs // 2 - 1)
+        def _():
+            q_share(b).wait_recv()
+            for i in range(own_heads):
+                q_buf[oc * own_heads + i] = q_recv[b % 2, i].astype(BF16)
+
+        head = 2 * ((j + c * (pairs // 2)) % pairs)
+        after = 2 * ((jnp.minimum(j + 1, pairs - 1) + c * (pairs // 2)) % pairs)
+
         def run(kb):
             stats = msg[b % 2, :, heads * head_dim:]
-            scores(2 * j + 1, 1, kb)
-            stats = one_head(b, 2 * j, 0, kb, stats)
-            scores(jnp.minimum(2 * j + 2, heads - 1), 0, kb)
-            msg[b % 2, :, heads * head_dim:] = one_head(b, 2 * j + 1, 1, kb, stats)
+            scores(head + 1, 1, kb)
+            stats = one_head(b, head, 0, kb, stats)
+            scores(after, 0, kb)
+            msg[b % 2, :, heads * head_dim:] = one_head(b, head + 1, 1, kb, stats)
 
         each_variant(b, run)
 
@@ -456,22 +507,11 @@
         kv_rows_copy(stages - 1, 0).wait()
         kv_rows_copy(stages - 1, 1).wait()
 
-    out_copy(stages - 1).wait()
-    for b in range(stages):
-        if b >= stages - 2:
-            m_share(b).wait_send()
-        for i in range(6):
-            m_x(b, i).wait_send()
-            m_y(b, i).wait_send()
-        for to in (1, -1):
-            g_first(b, to, 0, None).wait_send()
-            g_first(b, to, -to, 0 if to == 1 else 1).wait_send()
-            for du in range(4):
-                g_second(b, to, du, 0, None).wait_send()
-                g_second(b, to, du, -to, 0 if to == 1 else 1).wait_send()
-        for du in range(4):
-            for dv in range(4):
-                g_share(b, du, dv).wait_send()
+    out_copy(stages - 1, c).wait()
+    out_copy_2(stages - 1, oc).wait()
+    q_share(stages - 1).wait_send()
+    for b in range(stages - 2, stages):
+        m_share(b).wait_send()
 
 
 def attend_and_combine(mesh, write_at, hidden, w_query, w_key, w_value, norm_gain, q_gain, k_gain, cosine, sine, k_heads, v_heads, w_out):
@@ -496,17 +536,19 @@
         in_specs=[pl.BlockSpec(memory_space=pltpu.SMEM)] + [anywhere] * 4 + [vmem] * 3 + [anywhere] * 5,
         out_specs=(anywhere,) * 3,
         scratch_shapes=[
-            pltpu.VMEM(w_query.shape, BF16),
+            pltpu.VMEM((model, w_query.shape[1] // 2), BF16),
             pltpu.VMEM(w_key.shape, BF16),
             pltpu.VMEM(w_value.shape, BF16),
             pltpu.VMEM(w_out.shape, BF16),
             pltpu.VMEM((srows, model), BF16),
             pltpu.VMEM((srows, model), BF16),
-            pltpu.VMEM((2, srows, head_dim), F32),
-            pltpu.VMEM((2, srows, head_dim), F32),
+            pltpu.VMEM((2, srows, head_dim // 2), F32),
+            pltpu.VMEM((2, srows, head_dim // 2), F32),
             pltpu.VMEM(k_heads.shape, BF16),
             pltpu.VMEM(v_heads.shape, BF16),
             pltpu.VMEM((w_query.shape[1] // head_dim, srows, head_dim), BF16),
+            pltpu.VMEM((w_query.shape[1] // head_dim // 2, srows, head_dim), F32),
+            pltpu.VMEM((2, w_query.shape[1] // head_dim // 2, srows, head_dim), F32),
             pltpu.VMEM((srows, shard_len), F32),
             pltpu.VMEM((srows, shard_len), F32),
             pltpu.VMEM((srows, shard_len), BF16),
@@ -527,6 +569,7 @@
             pltpu.VMEM((STAGES, srows, model), F32),
             pltpu.VMEM((srows, model), BF16),
             dma((6,)),
+            dma((2, STAGES)),
             dma((STAGES, 2)),
             dma((STAGES,)),
             dma((STAGES,)),
@@ -536,7 +579,7 @@
             dma((STAGES, 32)),
             dma((STAGES, 16)),
             dma((STAGES, 16)),
-            dma((STAGES,)),
+            dma((STAGES, 2)),
         ],
         compiler_params=pltpu.CompilerParams(collective_id=0, has_side_effects=True, vmem_limit_bytes=67043328),
     )(write_at.reshape(1), hidden, w_query, w_key, w_value, norm_gain.reshape(1, model), q_gain.reshape(1, head_dim), k_gain.reshape(1, head_dim),

time: 147 us -> 137 us (0.932)
  Pallas kernels: 139 us -> 129 us
    pallas_call x1, Pallas kernels: 131 us -> 121 us  [attend_and_combine(): pl.pallas_call(functools.partial(group_kernel, mesh.shape['sp'] - 1, nx,...]
    sin x0 -> x1, other arithmetic: none -> 3.05 us  [rope_tables(): cosine, sine = (jnp.cos(angles), jnp.sin(angles))]
    neg x1 -> x0, other arithmetic: 1.9 us -> none  [rope_tables(): -sine]
where the time goes in v1:
time: 137 us
  Pallas kernels  129 us (94%)
  local copies, waits for them, and re-layouts  3.13 us (2%)
  other arithmetic  3.06 us (2%)
    pallas_call x1, Pallas kernels, attend_and_combine(): pl.pallas_call(functools.partial(group_kernel, mesh.shape['sp'] - 1, nx,...  121 us
    pallas_call x1, Pallas kernels, finish(): pl.pallas_call(functools.partial(finish_kernel, n_last, pieces), name='fi...  8.23 us
    transpose x1, local copies, waits for them, and re-layouts, local_step(): jnp.transpose(v_shard, (1, 0, 2))  3.13 us
    sin x1, other arithmetic, rope_tables(): cosine, sine = (jnp.cos(angles), jnp.sin(angles))  3.05 us

profile of v1, /device:TPU:97, one launch (start us, length us, event | category | flops | bytes accessed | tf_op | source)
XLA Modules:
  0.0 136.5 jit_solution(7939322497499043969)
XLA Ops:
  1.3 3.0 %multiply_sine_fusion = (f32[1024,64]{1,0:T(8,128)}, f32[1024,64]{1,0:T(8,128)}) fusion(f32[64]{0:T(128)S(1)} %multiply_power_fusion, f32[1024]{0:T(1024)S(1)} %add_convert_fusion), kind=kLoop, calls=%fused_computation.2 | loop fusion | flops 65536 | bytes 528640 | tf_op jit(solution)/shard_map/sin | solution.py:34
  4.4 3.1 %copy_bitcast_fusion = (bf16[2,2048,128]{2,1,0:T(8,128)(2,1)}, bf16[2,2048,128]{2,1,0:T(8,128)(2,1)}) fusion(bf16[2048,2,128]{2,1,0:T(2,128)(2,1)} %v_in.1, bf16[2048,2,128]{2,1,0:T(2,128)(2,1)} %k_in.1), kind=kLoop, calls=%fused_computation | loop fusion | bytes 4194304 | tf_op jit(solution)/shard_map/transpose | solution.py:654
  7.5 120.8 %attend_and_combine.1 = (bf16[1024,4096]{1,0:T(8,128)(2,1)}, bf16[1024,2,128]{2,1,0:T(2,128)(2,1)}, bf16[1024,2,128]{2,1,0:T(2,128)(2,1)}) custom-call(s32[1]{0:T(128)} %bitcast.1.at_ref, bf16[1024,4096]{1,0:T(8,128)(2,1)} %h_hbm.1, bf16[4096,1024]{1,0:T(8,128)(2,1)} %wq_hbm.1, bf16[4096,256]{1,0:T(8,128)(2,1)} %wk_hbm.1, bf16[4096,256]{1,0:T(8,128)(2,1)} %wv_hbm.1, ...), custom_call_target="tpu_custom_call" | custom-call | tf_op jit(solution)/shard_map/attend_and_combine/pallas_call | solution.py:532
  128.3 8.2 %finish.1 = (bf16[1024,4096]{1,0:T(8,128)(2,1)}, bf16[2048,2,128]{2,1,0:T(2,128)(2,1)}, bf16[2048,2,128]{2,1,0:T(2,128)(2,1)}) custom-call(s32[1]{0:T(128)} %bitcast.1.at_ref, bf16[1024,4096]{1,0:T(8,128)(2,1)} %get-tuple-element.6.out_in, bf16[2048,2,128]{2,1,0:T(2,128)(2,1)} %k_in.1, bf16[2048,2,128]{2,1,0:T(2,128)(2,1)} %v_in.1, ...), custom_call_target="tpu_custom_call" | custom-call | tf_op jit(solution)/shard_map/finish/pallas_call | solution.py:630
  (2 shorter events, 0.0 us)

commit v2 on v1

--- a/solution.py
+++ b/solution.py
@@ -13,9 +13,9 @@
 LANES = 128
 STAGES = 4
 STEP_AT = (
-    (5, 10, 15, 20), (6, 11, 16, 21), (9, 13, 20, 22), (11, 15, 22, 25),
-    (13, 16, 24, 27), (15, 20, 26, 29), (16, 22, 28, 30), (19, 25, 30, 31),
-    (22, 27, 31, 33), (23, 29, 32, 34), (24, 30, 33, 35),
+    (5, 10, 16, 20), (6, 11, 17, 21), (8, 13, 21, 22), (11, 15, 22, 24),
+    (13, 16, 23, 25), (15, 19, 26, 27), (16, 22, 28, 29), (18, 24, 30, 31),
+    (23, 25, 32, 33), (28, 31, 34, 35), (31, 34, 36, 37),
 )
 F32 = jnp.float32
 BF16 = jnp.bfloat16
@@ -27,12 +27,14 @@
     return values * lax.rsqrt(mean_sq + NORM_EPS) * gain
 
 
-def rope_tables(positions, head_dim):
+def rope_tables(first_pos, chunk_len, head_dim):
     half_dim = head_dim // 2
     inv_freq = ROPE_BASE ** (-2.0 * jnp.arange(half_dim, dtype=F32) / head_dim)
-    angles = positions.astype(F32)[:, None] * inv_freq[None, :]
-    cosine, sine = jnp.cos(angles), jnp.sin(angles)
-    return cosine, sine
+    row = lax.broadcasted_iota(jnp.int32, (chunk_len // 2, head_dim), 0)
+    lane = lax.broadcasted_iota(jnp.int32, (chunk_len // 2, head_dim), 1)
+    positions = first_pos + row + jnp.where(lane < half_dim, 0, chunk_len // 2)
+    angles = positions.astype(F32) * jnp.concatenate([inv_freq, inv_freq])[None, :]
+    return jnp.cos(angles), jnp.sin(angles)
 
 
 def merge(a, b, heads):
@@ -114,7 +116,7 @@
 
     def table_load(b, i):
         src, dst = ((cos_hbm, cos_buf), (sin_hbm, sin_buf))[i]
-        return pltpu.make_async_copy(src.at[ds(b * srows, srows)], dst.at[b % 2], table_sem.at[b, i])
+        return pltpu.make_async_copy(src.at[ds((b % (stages // 2)) * srows, srows)], dst.at[b % 2], table_sem.at[b, i])
 
     h_load(0).start()
     for i in range(2):
@@ -134,6 +136,18 @@
     barrier = pltpu.get_barrier_semaphore()
     for dev in (partner, right, left, up, down):
         pl.semaphore_signal(barrier, inc=1, device_id=dev, device_id_type=MESH)
+
+    def normalise(b):
+        h_load(b).wait()
+
+        @pl.loop(0, srows // 16, unroll=2)
+        def _(r):
+            rows = ds(r * 16, 16)
+            hf = h_buf[rows].astype(F32)
+            mean_sq = jnp.mean(hf * hf, axis=-1, keepdims=True)
+            x_buf[rows] = (hf * lax.rsqrt(mean_sq + NORM_EPS) * gain_ref[...]).astype(BF16)
+
+    normalise(0)
     pl.semaphore_wait(barrier, 5)
 
     def copy(src, dst, ssem, rsem, dev):
@@ -377,14 +391,9 @@
         def _():
             m_share(b - 2).wait_send()
 
-        h_load(b).wait()
-
-        @pl.loop(0, srows // 16, unroll=2)
-        def _(r):
-            rows = ds(r * 16, 16)
-            hf = h_buf[rows].astype(F32)
-            mean_sq = jnp.mean(hf * hf, axis=-1, keepdims=True)
-            x_buf[rows] = (hf * lax.rsqrt(mean_sq + NORM_EPS) * gain_ref[...]).astype(BF16)
+        @pl.when(b > 0)
+        def _():
+            normalise(b)
 
         @pl.when(b + 1 < stages)
         def _():
@@ -395,8 +404,10 @@
         table_load(b, 0).wait()
         table_load(b, 1).wait()
 
-        cosine, sine = cos_buf[b % 2], sin_buf[b % 2]
-        cosine, sine = jnp.concatenate([cosine, cosine], axis=1), jnp.concatenate([-sine, sine], axis=1)
+        low = lane < head_dim // 2
+        here = low == (b < stages // 2)
+        cosine, sine = (jnp.where(here, table[b % 2], pltpu.roll(table[b % 2], head_dim // 2, 1)) for table in (cos_buf, sin_buf))
+        sine = jnp.where(low, -sine, sine)
 
         def rope(one):
             return one * cosine + pltpu.roll(one, head_dim // 2, 1) * sine
@@ -542,8 +553,8 @@
             pltpu.VMEM(w_out.shape, BF16),
             pltpu.VMEM((srows, model), BF16),
             pltpu.VMEM((srows, model), BF16),
-            pltpu.VMEM((2, srows, head_dim // 2), F32),
-            pltpu.VMEM((2, srows, head_dim // 2), F32),
+            pltpu.VMEM((2, srows, head_dim), F32),
+            pltpu.VMEM((2, srows, head_dim), F32),
             pltpu.VMEM(k_heads.shape, BF16),
             pltpu.VMEM(v_heads.shape, BF16),
             pltpu.VMEM((w_query.shape[1] // head_dim, srows, head_dim), BF16),
@@ -625,7 +636,7 @@
 
 
 def finish(n_last, write_at, out, k_shard, v_shard, k_new, v_new):
-    pieces = 8
+    pieces = 16
     anywhere = pl.BlockSpec(memory_space=pl.ANY)
     return pl.pallas_call(
         functools.partial(finish_kernel, n_last, pieces),
@@ -648,7 +659,7 @@
         chunk_len, model_dim = hidden.shape
         shard_len, kv_local, head_dim = k_shard.shape
         first_pos = start_pos[0]
-        cosine, sine = rope_tables(first_pos + jnp.arange(chunk_len, dtype=jnp.int32), head_dim)
+        cosine, sine = rope_tables(first_pos, chunk_len, head_dim)
 
         write_at = first_pos - n_last * shard_len
         k_heads, v_heads = jnp.transpose(k_shard, (1, 0, 2)), jnp.transpose(v_shard, (1, 0, 2))

time: 137 us -> 133 us (0.971)
  Pallas kernels: 129 us -> 127 us
    pallas_call x1, Pallas kernels: 121 us -> 119 us  [attend_and_combine(): pl.pallas_call(functools.partial(group_kernel, mesh.shape['sp'] - 1, nx,...]
where the time goes in v2:
time: 133 us
  Pallas kernels  127 us (95%)
  local copies, waits for them, and re-layouts  3.13 us (2%)
  other arithmetic  1.92 us (1%)
    pallas_call x1, Pallas kernels, attend_and_combine(): pl.pallas_call(functools.partial(group_kernel, mesh.shape['sp'] - 1, nx,...  119 us
    pallas_call x1, Pallas kernels, finish(): pl.pallas_call(functools.partial(finish_kernel, n_last, pieces), name='fi...  8.2 us
    transpose x1, local copies, waits for them, and re-layouts, local_step(): jnp.transpose(v_shard, (1, 0, 2))  3.13 us

profile of v2, /device:TPU:97, one launch (start us, length us, event | category | flops | bytes accessed | tf_op | source)
XLA Modules:
  0.0 133.3 jit_solution(15511789722407789299)
XLA Ops:
  1.3 0.1 pad_maximum_fusion
  1.4 1.8 %fusion = (f32[512,128]{1,0:T(8,128)}, f32[512,128]{1,0:T(8,128)}) fusion(f32[128]{0:T(128)S(1)} %pad_maximum_fusion, s32[128]{0:T(128)S(1)} %compare_select_fusion, s32[512]{0:T(512)S(1)} %iota_add_fusion), kind=kLoop, calls=%fused_computation.3 | loop fusion | flops 196608 | bytes 527360 | tf_op jit(solution)/shard_map/sin | solution.py:37
  3.2 3.1 %copy_bitcast_fusion = (bf16[2,2048,128]{2,1,0:T(8,128)(2,1)}, bf16[2,2048,128]{2,1,0:T(8,128)(2,1)}) fusion(bf16[2048,2,128]{2,1,0:T(2,128)(2,1)} %v_in.1, bf16[2048,2,128]{2,1,0:T(2,128)(2,1)} %k_in.1), kind=kLoop, calls=%fused_computation | loop fusion | bytes 4194304 | tf_op jit(solution)/shard_map/transpose | solution.py:665
  6.3 118.8 %attend_and_combine.1 = (bf16[1024,4096]{1,0:T(8,128)(2,1)}, bf16[1024,2,128]{2,1,0:T(2,128)(2,1)}, bf16[1024,2,128]{2,1,0:T(2,128)(2,1)}) custom-call(s32[1]{0:T(128)} %bitcast.1.at_ref, bf16[1024,4096]{1,0:T(8,128)(2,1)} %h_hbm.1, bf16[4096,1024]{1,0:T(8,128)(2,1)} %wq_hbm.1, bf16[4096,256]{1,0:T(8,128)(2,1)} %wk_hbm.1, bf16[4096,256]{1,0:T(8,128)(2,1)} %wv_hbm.1, ...), custom_call_target="tpu_custom_call" | custom-call | tf_op jit(solution)/shard_map/attend_and_combine/pallas_call | solution.py:543
  125.1 8.2 %finish.1 = (bf16[1024,4096]{1,0:T(8,128)(2,1)}, bf16[2048,2,128]{2,1,0:T(2,128)(2,1)}, bf16[2048,2,128]{2,1,0:T(2,128)(2,1)}) custom-call(s32[1]{0:T(128)} %bitcast.1.at_ref, bf16[1024,4096]{1,0:T(8,128)(2,1)} %get-tuple-element.6.out_in, bf16[2048,2,128]{2,1,0:T(2,128)(2,1)} %k_in.1, bf16[2048,2,128]{2,1,0:T(2,128)(2,1)} %v_in.1, ...), custom_call_target="tpu_custom_call" | custom-call | tf_op jit(solution)/shard_map/finish/pallas_call | solution.py:641
  (3 shorter events, 0.0 us)
